TPU v7x, 32 devices: a whole 2x2x4 slice. The times are simulated.
32 devices in a mesh: dp: 4 (over y, x), fsdp: 8 (over z, core).
Axes of the slice: x: 2, y: 2, z: 4, core: 2. Of those that a mesh axis runs over, the one named last changes fastest.
Arguments:
- tokens: bfloat16 [32768, 768], P(('dp', 'fsdp')), may hold values from -6 to 6
- cotangent: bfloat16 [32768, 768], P(('dp', 'fsdp')), may hold values from -6 to 6
- lengths: int32 [64], P(('dp', 'fsdp')), may hold values from 128 to 512, as said below
- mb_count: int32 [4], replicated, may hold values from 1 to 2, as said below
- query_weight: bfloat16 [768, 768], P('fsdp'), may hold values from -0.21875 to 0.21875
- query_bias: bfloat16 [768], P('fsdp'), may hold values from -1.5 to 1.5
- key_weight: bfloat16 [768, 768], P('fsdp'), may hold values from -0.21875 to 0.21875
- value_weight: bfloat16 [768, 768], P('fsdp'), may hold values from -0.21875 to 0.21875
- value_bias: bfloat16 [768], P('fsdp'), may hold values from -1.5 to 1.5
- output_weight: bfloat16 [768, 768], P('fsdp'), may hold values from -1.75 to 1.75
- output_bias: bfloat16 [768], P('fsdp'), may hold values from -1.5 to 1.5
- first_gain: bfloat16 [768], P('fsdp'), may hold values from 0.5 to 1.5
- first_shift: bfloat16 [768], P('fsdp'), may hold values from -1.5 to 1.5
- up_weight: bfloat16 [768, 3072], P('fsdp'), may hold values from -0.21875 to 0.21875
- up_bias: bfloat16 [3072], P('fsdp'), may hold values from -1.5 to 1.5
- down_weight: bfloat16 [3072, 768], P('fsdp'), may hold values from -0.109375 to 0.109375
- down_bias: bfloat16 [768], P('fsdp'), may hold values from -1.5 to 1.5
- second_gain: bfloat16 [768], P('fsdp'), may hold values from 0.5 to 1.5
- second_shift: bfloat16 [768], P('fsdp'), may hold values from -1.5 to 1.5
Outputs:
- layer_out: bfloat16 [32768, 768], P(('dp', 'fsdp'))
- tokens_grad: bfloat16 [32768, 768], P(('dp', 'fsdp'))
- query_weight_grad: float32 [768, 768], P('fsdp')
- query_bias_grad: float32 [768], P('fsdp')
- key_weight_grad: float32 [768, 768], P('fsdp')
- value_weight_grad: float32 [768, 768], P('fsdp')
- value_bias_grad: float32 [768], P('fsdp')
- output_weight_grad: float32 [768, 768], P('fsdp')
- output_bias_grad: float32 [768], P('fsdp')
- first_gain_grad: float32 [768], P('fsdp')
- first_shift_grad: float32 [768], P('fsdp')
- up_weight_grad: float32 [768, 3072], P('fsdp')
- up_bias_grad: float32 [3072], P('fsdp')
- down_weight_grad: float32 [3072, 768], P('fsdp')
- down_bias_grad: float32 [768], P('fsdp')
- second_gain_grad: float32 [768], P('fsdp')
- second_shift_grad: float32 [768], P('fsdp')
Inputs may be any that keep to these rules, and one draw needn't show every extreme that they name: `lengths`: keys at positions at or past a sequence's length are padding; some sequence has all 512 keys valid and some has 128. Data group g runs slots 0 .. mb_count[g] - 1 of each of its devices; some group runs all 2 and some runs one.
All inputs are finite; a program needn't handle non-finite values.
Results may differ from a plain program's by a relative error of at most 0.02.
Values may be sent and summed in bfloat16 or wider, within the bound.
A program may use at most 144 MiB of HBM per device.

v0:
```python
import jax
import jax.numpy as jnp
from jax import lax
from jax.sharding import PartitionSpec as P

HEADS = 12
MB_CAP = 2
norm_epsilon = 1e-05


def for_sending(shard):

    def short(part):
        return part.astype(jnp.bfloat16) if part.dtype == jnp.float32 else part

    return jax.tree.map(short, shard)


def gelu_exact(values):
    return jax.nn.gelu(values, approximate=False)


def layer_norm(hidden, gain, shift):
    centre = hidden - jnp.mean(hidden, axis=-1, keepdims=True)
    inverse = lax.rsqrt(jnp.mean(centre * centre, axis=-1, keepdims=True) + norm_epsilon)
    normed = centre * inverse
    return (normed * gain.astype(jnp.float32) + shift.astype(jnp.float32), normed, inverse)


def norm_backward(grad_out, normed, inverse, gain):
    scaled = grad_out * gain.astype(jnp.float32)
    inner = scaled - jnp.mean(scaled, axis=-1, keepdims=True)
    inner = inner - normed * jnp.mean(scaled * normed, axis=-1, keepdims=True)
    return inverse * inner


def to_heads(values, seq_count, heads):
    width = values.shape[1]
    shaped = values.reshape(seq_count, -1, heads, width // heads)
    return jnp.transpose(shaped, (0, 2, 3, 1))


def from_heads(values):
    shaped = jnp.transpose(values, (0, 3, 1, 2))
    return shaped.reshape(-1, values.shape[1] * values.shape[2])


def masked_scores(query_cols, key_cols, length):
    factor = query_cols.shape[1] ** (-0.5)
    scores = (
        jnp.einsum("hdq,hdk->hqk", query_cols, key_cols, preferred_element_type=jnp.float32)
        * factor
    )
    visible = jnp.arange(key_cols.shape[2], dtype=jnp.int32) < length
    masked = jnp.where(visible[None, None, :], scores, -1000000000.0)
    return (masked, factor)


def attend_forward(query_cols, key_cols, value_cols, length):
    scores, factor = masked_scores(query_cols, key_cols, length)
    top = jnp.max(scores, axis=-1, keepdims=True)
    expo = jnp.exp(scores - top)
    total = jnp.sum(expo, axis=-1, keepdims=True)
    probs = (expo / total).astype(jnp.bfloat16)
    log_total = top[..., 0] + jnp.log(total[..., 0])
    context = jnp.einsum("hdk,hqk->hdq", value_cols, probs, preferred_element_type=jnp.float32)
    return (context.astype(jnp.bfloat16), log_total)


def attend_backward(query_cols, key_cols, value_cols, length, log_total, grad_cols):
    scores, factor = masked_scores(query_cols, key_cols, length)
    probs = jnp.exp(scores - log_total[..., None])
    grad_probs = jnp.einsum(
        "hdq,hdk->hqk", grad_cols, value_cols, preferred_element_type=jnp.float32
    )
    grad_values = jnp.einsum(
        "hqk,hdq->hdk", probs.astype(jnp.bfloat16), grad_cols, preferred_element_type=jnp.float32
    ).astype(jnp.bfloat16)
    delta = jnp.sum(grad_probs * probs, axis=-1, keepdims=True)
    grad_scores = (probs * (grad_probs - delta)).astype(jnp.bfloat16)
    grad_queries = (
        factor
        * jnp.einsum("hqk,hdk->hdq", grad_scores, key_cols, preferred_element_type=jnp.float32)
    ).astype(jnp.bfloat16)
    grad_keys = (
        factor
        * jnp.einsum("hqk,hdq->hdk", grad_scores, query_cols, preferred_element_type=jnp.float32)
    ).astype(jnp.bfloat16)
    return (grad_queries, grad_keys, grad_values)


def project(left, right):
    return jnp.dot(left, right, preferred_element_type=jnp.float32)


def project_back(left, right):
    return jnp.einsum("rc,dc->rd", left, right, preferred_element_type=jnp.float32)


def weight_grad(left, right):
    return jnp.einsum("rc,rd->cd", left, right, preferred_element_type=jnp.float32)


def column_sum(values):
    return jnp.sum(values.astype(jnp.float32), axis=0)


def slot_forward(rows, weights, seq_lengths, heads):
    (
        w_query,
        b_query,
        w_key,
        w_value,
        b_value,
        w_output,
        b_output,
        gain_one,
        shift_one,
        w_up,
        b_up,
        w_down,
        b_down,
        gain_two,
        shift_two,
    ) = weights
    seq_count = seq_lengths.shape[0]
    queries = (project(rows, w_query) + b_query.astype(jnp.float32)).astype(jnp.bfloat16)
    key_rows = project(rows, w_key).astype(jnp.bfloat16)
    value_rows = (project(rows, w_value) + b_value.astype(jnp.float32)).astype(jnp.bfloat16)
    query_cols = to_heads(queries, seq_count, heads)
    key_cols = to_heads(key_rows, seq_count, heads)
    value_cols = to_heads(value_rows, seq_count, heads)

    def one_sequence(item):
        return attend_forward(item[0], item[1], item[2], item[3])

    context_cols, log_total = lax.map(one_sequence, (query_cols, key_cols, value_cols, seq_lengths))
    context = from_heads(context_cols)
    first_sum = rows.astype(jnp.float32) + project(context, w_output) + b_output.astype(jnp.float32)
    middle, normed_one, inverse_one = layer_norm(first_sum, gain_one, shift_one)
    middle_low = middle.astype(jnp.bfloat16)
    upper = project(middle_low, w_up) + b_up.astype(jnp.float32)
    active = gelu_exact(upper).astype(jnp.bfloat16)
    second_sum = middle + project(active, w_down) + b_down.astype(jnp.float32)
    result, normed_two, inverse_two = layer_norm(second_sum, gain_two, shift_two)
    saved = (
        query_cols,
        key_cols,
        value_cols,
        log_total,
        context,
        normed_one,
        inverse_one,
        middle_low,
        upper,
        active,
        normed_two,
        inverse_two,
    )
    return (result, saved)


def slot_backward(rows, grad_out, saved, weights, seq_lengths, heads):
    (
        w_query,
        b_query,
        w_key,
        w_value,
        b_value,
        w_output,
        b_output,
        gain_one,
        shift_one,
        w_up,
        b_up,
        w_down,
        b_down,
        gain_two,
        shift_two,
    ) = weights
    (
        query_cols,
        key_cols,
        value_cols,
        log_total,
        context,
        normed_one,
        inverse_one,
        middle_low,
        upper,
        active,
        normed_two,
        inverse_two,
    ) = saved
    seq_count = seq_lengths.shape[0]
    gain_two_grad = jnp.sum(grad_out * normed_two, axis=0)
    shift_two_grad = jnp.sum(grad_out, axis=0)
    grad_second = norm_backward(grad_out, normed_two, inverse_two, gain_two)
    grad_down = grad_second.astype(jnp.bfloat16)
    down_bias_grad = column_sum(grad_down)
    down_weight_grad = weight_grad(active, grad_down)
    grad_active = project_back(grad_down, w_down)
    gelu_value, gelu_pull = jax.vjp(gelu_exact, upper)
    grad_upper = gelu_pull(grad_active)[0].astype(jnp.bfloat16)
    up_bias_grad = column_sum(grad_upper)
    up_weight_grad = weight_grad(middle_low, grad_upper)
    grad_middle = grad_second + project_back(grad_upper, w_up)
    gain_one_grad = jnp.sum(grad_middle * normed_one, axis=0)
    shift_one_grad = jnp.sum(grad_middle, axis=0)
    grad_first = norm_backward(grad_middle, normed_one, inverse_one, gain_one)
    grad_branch = grad_first.astype(jnp.bfloat16)
    output_bias_grad = column_sum(grad_branch)
    output_weight_grad = weight_grad(context, grad_branch)
    grad_context = project_back(grad_branch, w_output).astype(jnp.bfloat16)
    grad_cols = to_heads(grad_context, seq_count, heads)

    def one_sequence(item):
        return attend_backward(item[0], item[1], item[2], item[3], item[4], item[5])

    grad_query_cols, grad_key_cols, grad_value_cols = lax.map(
        one_sequence, (query_cols, key_cols, value_cols, seq_lengths, log_total, grad_cols)
    )
    grad_queries = from_heads(grad_query_cols)
    grad_keys = from_heads(grad_key_cols)
    grad_values = from_heads(grad_value_cols)
    grads = (
        weight_grad(rows, grad_queries),
        column_sum(grad_queries),
        weight_grad(rows, grad_keys),
        weight_grad(rows, grad_values),
        column_sum(grad_values),
        output_weight_grad,
        output_bias_grad,
        gain_one_grad,
        shift_one_grad,
        up_weight_grad,
        up_bias_grad,
        down_weight_grad,
        down_bias_grad,
        gain_two_grad,
        shift_two_grad,
    )
    grad_rows = grad_first + project_back(grad_queries, w_query) + project_back(grad_keys, w_key)
    grad_rows = grad_rows + project_back(grad_values, w_value)
    return (grad_rows.astype(jnp.bfloat16), grads)


def local(
    tokens,
    cotangent,
    lengths,
    mb_count,
    query_weight,
    query_bias,
    key_weight,
    value_weight,
    value_bias,
    output_weight,
    output_bias,
    first_gain,
    first_shift,
    up_weight,
    up_bias,
    down_weight,
    down_bias,
    second_gain,
    second_shift,
):
    shards = (
        query_weight,
        query_bias,
        key_weight,
        value_weight,
        value_bias,
        output_weight,
        output_bias,
        first_gain,
        first_shift,
        up_weight,
        up_bias,
        down_weight,
        down_bias,
        second_gain,
        second_shift,
    )
    group_size = lax.axis_size("fsdp")
    slot_rows = tokens.shape[0] // MB_CAP
    slot_seqs = lengths.shape[0] // MB_CAP
    group_count = mb_count[lax.axis_index("dp")]
    totals = tuple(
        (jnp.zeros((group_size * item.shape[0],) + item.shape[1:], jnp.float32) for item in shards)
    )
    results = []
    input_grads = []
    for slot_index in range(MB_CAP):
        gathered = (
            lax.all_gather(shards[0], "fsdp", axis=0, tiled=True),
            lax.all_gather(shards[1], "fsdp", axis=0, tiled=True),
            lax.all_gather(shards[2], "fsdp", axis=0, tiled=True),
            lax.all_gather(shards[3], "fsdp", axis=0, tiled=True),
            lax.all_gather(shards[4], "fsdp", axis=0, tiled=True),
            lax.all_gather(shards[5], "fsdp", axis=0, tiled=True),
            lax.all_gather(shards[6], "fsdp", axis=0, tiled=True),
            lax.all_gather(shards[7], "fsdp", axis=0, tiled=True),
            lax.all_gather(shards[8], "fsdp", axis=0, tiled=True),
            lax.all_gather(shards[9], "fsdp", axis=0, tiled=True),
            lax.all_gather(shards[10], "fsdp", axis=0, tiled=True),
            lax.all_gather(shards[11], "fsdp", axis=0, tiled=True),
            lax.all_gather(shards[12], "fsdp", axis=0, tiled=True),
            lax.all_gather(shards[13], "fsdp", axis=0, tiled=True),
            lax.all_gather(shards[14], "fsdp", axis=0, tiled=True),
        )
        rows = tokens[slot_index * slot_rows : (slot_index + 1) * slot_rows]
        seq_lengths = lengths[slot_index * slot_seqs : (slot_index + 1) * slot_seqs]
        result, saved = slot_forward(rows, gathered, seq_lengths, HEADS)
        results.append(result.astype(jnp.bfloat16))
        grad_out = cotangent[slot_index * slot_rows : (slot_index + 1) * slot_rows].astype(
            jnp.float32
        )

        def run_backward(carried):
            grad_rows, grads = slot_backward(rows, grad_out, saved, gathered, seq_lengths, HEADS)
            return (grad_rows, tuple((total + piece for total, piece in zip(carried, grads))))

        def skip_backward(carried):
            return (jnp.zeros_like(rows), carried)

        grad_rows, totals = lax.cond(slot_index < group_count, run_backward, skip_backward, totals)
        input_grads.append(grad_rows)
    pieces = jax.tree.map(
        lambda part: part.astype(jnp.float32),
        lax.psum_scatter(for_sending(totals), "fsdp", scatter_dimension=0, tiled=True),
    )
    summed = jax.tree.map(
        lambda part: part.astype(jnp.float32), lax.psum(for_sending(pieces), "dp")
    )
    return (jnp.concatenate(results, axis=0), jnp.concatenate(input_grads, axis=0)) + tuple(summed)


def solution(mesh):
    return jax.shard_map(
        local,
        mesh=mesh,
        in_specs=(
            P(("dp", "fsdp"), None),
            P(("dp", "fsdp"), None),
            P(("dp", "fsdp")),
            P(),
            P("fsdp", None),
            P("fsdp"),
            P("fsdp", None),
            P("fsdp", None),
            P("fsdp"),
            P("fsdp", None),
            P("fsdp"),
            P("fsdp"),
            P("fsdp"),
            P("fsdp", None),
            P("fsdp"),
            P("fsdp", None),
            P("fsdp"),
            P("fsdp"),
            P("fsdp"),
        ),
        out_specs=(
            P(("dp", "fsdp"), None),
            P(("dp", "fsdp"), None),
            P("fsdp", None),
            P("fsdp"),
            P("fsdp", None),
            P("fsdp", None),
            P("fsdp"),
            P("fsdp", None),
            P("fsdp"),
            P("fsdp"),
            P("fsdp"),
            P("fsdp", None),
            P("fsdp"),
            P("fsdp", None),
            P("fsdp"),
            P("fsdp"),
            P("fsdp"),
        ),
        check_vma=False,
    )
```

profile of v0, /device:TPU:0, one launch (start us, length us, event | category | flops | bytes accessed | tf_op | source)
XLA Modules:
  0.0 763.2 jit_solution(17119618371949956671)
XLA Ops:
  21.6 31.4 %all-reduce.18 = (bf16[768]{0:T(1024)(128)(2,1)S(1)}, bf16[768]{0:T(1024)(128)(2,1)S(1)}, bf16[768]{0:T(1024)(128)(2,1)S(1)}, bf16[768]{0:T(1024)(128)(2,1)S(1)}...) all-reduce(bf16[768]{0:T(1024)(128)(2,1)S(1)} %dynamic-update-slice, ...), channel_id=1, replica_groups=mesh['dp'=4,'fsdp'=8] {'fsdp'}, use_global_device_ids=true, to_apply=%add | all-reduce | flops 5376 | bytes 21504
  55.7 12.7 %all-gather = bf16[8,1,384]{2,1,0:T(2,128)(2,1)S(1)} all-gather(bf16[1,1,384]{2,1,0:T(2,128)(2,1)S(1)} %reshape.281), channel_id=1, replica_groups=mesh['dp'=4,'fsdp'=8] {'fsdp'}, dimensions={0}, use_global_device_ids=true | all-gather | bytes 6912 | tf_op jit(solution)/shard_map/all_gather | solution.py:307
  69.1 4.1 slice_convert_fusion
  78.2 5.4 all-gather.12.cloned.1.call-done
  92.0 4.5 fusion.97
  96.5 11.1 %all-gather.14.cloned.1.call-done = bf16[768,768]{1,0:T(8,128)(2,1)} async-done(((bf16[96,768]{1,0:T(8,128)(2,1)}), bf16[768,768]{1,0:T(8,128)(2,1)}) %all-gather.14.cloned.1.call-update) | async-done | bytes 1179664 | tf_op jit(solution)/shard_map/all_gather | solution.py:302
  110.3 3.4 add_convert_fusion.4
  118.6 3.5 convolution_convert_fusion.2
  123.9 3.1 fusion.71
  129.6 3.3 fusion.96
  136.6 23.4 %all-gather.16.cloned.1.call-done = bf16[768,3072]{1,0:T(8,128)(2,1)} async-done(((bf16[96,3072]{1,0:T(8,128)(2,1)}), bf16[768,3072]{1,0:T(8,128)(2,1)}) %all-gather.16.cloned.1.call-update) | async-done | bytes 4718608 | tf_op jit(solution)/shard_map/all_gather | solution.py:306
  160.0 18.8 %fusion.76 = (bf16[512,3072]{1,0:T(8,128)(2,1)}, f32[512,3072]{1,0:T(8,128)}) fusion(f32[3072]{0:T(1024)S(1)} %bitcast.279, bf16[512,768]{1,0:T(8,128)(2,1)} %get-tuple-element.852, bf16[768,3072]{1,0:T(8,128)(2,1)} %all-gather.16.cloned.1.call-done), kind=kOutput, calls=%fused_computation.162 | convolution fusion | flops 2519728128 | bytes 14954496 | tf_op jit(solution)/shard_map/dot_general | solution.py:93
  178.7 32.7 %all-gather.18.cloned.1.call-done = bf16[3072,768]{1,0:T(8,128)(2,1)} async-done(((bf16[384,768]{1,0:T(8,128)(2,1)}), bf16[3072,768]{1,0:T(8,128)(2,1)}) %all-gather.18.cloned.1.call-update) | async-done | bytes 4718608 | tf_op jit(solution)/shard_map/all_gather | solution.py:308
  211.5 6.1 fusion.115
  218.3 18.2 %fusion.79 = (bf16[512,3072]{1,0:T(8,128)(2,1)S(1)}, f32[512,3072]{1,0:T(8,128)}) fusion(f32[3072]{0:T(1024)S(1)} %bitcast.280, bf16[512,768]{1,0:T(8,128)(2,1)S(1)} %copy-done.50, bf16[768,3072]{1,0:T(8,128)(2,1)S(1)} %copy-done.97), kind=kOutput, calls=%fused_computation.165 | convolution fusion | flops 2519728128 | bytes 14954496 | tf_op jit(solution)/shard_map/dot_general | solution.py:93
  241.4 90.8 %conditional.2 = (bf16[512,768]{1,0:T(8,128)(2,1)}, f32[768,768]{0,1:T(8,128)S(1)}, f32[768]{0:T(1024)S(1)}, f32[768,768]{0,1:T(8,128)}, f32[768,768]{0,1:T(8,12...) conditional(s32[]{:T(128)} %bitcast.104, () %tuple.36, ...), branch_computations={%region_12.13_spmd, %region_13.28_spmd} | conditional | flops 16691619840 | bytes 337698560 | solution.py:328
  241.6 6.4 fusion.22
  249.7 17.9 %convert_reduce_fusion = (f32[3072]{0:T(1024)S(1)}, bf16[512,3072]{1,0:T(8,128)(2,1)S(1)}) fusion(f32[512,3072]{1,0:T(8,128)S(1)} %get-tuple-element.439, bf16[3072,768]{1,0:T(8,128)(2,1)S(1)} %get-tuple-element.440, f32[512,768]{1,0:T(8,128)S(1)} %get-tuple-element.845), kind=kOutput, calls=%fused_computation.10 | convolution fusion | flops 2532701184 | bytes 15740928 | tf_op jit(solution)/shard_map/cond/branch_1_fun/rc,dc->rd/dot_general | solution.py:97
  275.2 11.7 %multiply_reduce_fusion = (f32[12,512]{1,0:T(8,128)S(1)}, f32[12,512,512]{1,2,0:T(8,128)}) fusion(f32[12,512,512]{1,2,0:T(8,128)} %fusion.22, f32[12,512]{1,0:T(8,128)S(1)} %log_add_fusion, pred[512]{0:T(512)(128)(4,1)S(1)} %iota_compare_fusion, bf16[12,64,512]{2,1,0:T(8,128)(2,1)} %bitcast.259, bf16[1,12,64,512]{3,2,1,0:T(8,128)(2,1)S(1)} %copy-done.41), kind=kOutput, calls=%fused_computation.1 | convolution fusion | flops 418375680 | bytes 26788352 | tf_op jit(solution)/shard_map/cond/branch_1_fun/while/body/eval_jaxpr/hdq,hdk->hqk/dot_general | solution.py:73
  288.0 7.4 multiply_convert_fusion
  301.5 3.2 convert_reduce_fusion.3
  307.4 3.6 convolution_bitcast_fusion.4
  311.0 3.6 convolution_bitcast_fusion.3
  314.6 3.8 convolution_bitcast_fusion.2
  318.5 8.4 %convolution_bitcast_fusion.1 = f32[768,3072]{0,1:T(8,128)} fusion(bf16[512,3072]{1,0:T(8,128)(2,1)} %copy-done.106, bf16[512,768]{1,0:T(8,128)(2,1)} %get-tuple-element.456), kind=kOutput, calls=%fused_computation.29 | convolution fusion | flops 2415919104 | bytes 13369344 | tf_op jit(solution)/shard_map/cond/branch_1_fun/rc,rd->cd/dot_general | solution.py:101
  326.9 5.0 convolution_bitcast_fusion
  332.8 99.3 %conditional.3 = (bf16[512,768]{1,0:T(8,128)(2,1)}, f32[768,768]{0,1:T(8,128)S(1)}, f32[768]{0:T(1024)S(1)}, f32[768,768]{0,1:T(8,128)}, f32[768,768]{0,1:T(8,12...) conditional(s32[]{:T(128)} %bitcast.110, ...), branch_computations={%region_28.29_spmd, %region_29.44_spmd} | conditional | flops 16698708992 | bytes 455893312 | solution.py:328
  332.9 7.7 %fusion.57 = f32[12,512,512]{1,2,0:T(8,128)} fusion(bf16[1,12,64,512]{3,2,1,0:T(8,128)(2,1)S(1)} %get-tuple-element.487, bf16[1,12,64,512]{3,2,1,0:T(8,128)(2,1)} %get-tuple-element.486), kind=kOutput, calls=%fused_computation.129 | convolution fusion | flops 402653184 | bytes 14155776 | tf_op jit(solution)/shard_map/cond/branch_1_fun/while/body/eval_jaxpr/hdq,hdk->hqk/dot_general | solution.py:51
  343.5 17.8 %convert_reduce_fusion.5 = (f32[3072]{0:T(1024)S(1)}, bf16[512,3072]{1,0:T(8,128)(2,1)S(1)}) fusion(f32[512,3072]{1,0:T(8,128)S(1)} %copy-done.107, bf16[3072,768]{1,0:T(8,128)(2,1)S(1)} %bitcast.290, f32[512,768]{1,0:T(8,128)S(1)} %get-tuple-element.849), kind=kOutput, calls=%fused_computation.86 | convolution fusion | flops 2532701184 | bytes 15740928 | tf_op jit(solution)/shard_map/cond/branch_1_fun/rc,dc->rd/dot_general | solution.py:97
  369.9 11.8 %multiply_reduce_fusion.7 = (f32[12,512]{1,0:T(8,128)S(1)}, f32[12,512,512]{1,2,0:T(8,128)}) fusion(f32[12,512,512]{1,2,0:T(8,128)} %fusion.57, f32[12,512]{1,0:T(8,128)S(1)} %log_add_fusion.1, pred[512]{0:T(512)(128)(4,1)S(1)} %iota_compare_fusion.1, bf16[12,64,512]{2,1,0:T(8,128)(2,1)} %bitcast.261, bf16[1,12,64,512]{3,2,1,0:T(8,128)(2,1)} %get-tuple-element.491), kind=kOutput, calls=%fused_computation.75 | convolution fusion | flops 418375680 | bytes 26788352 | tf_op jit(solution)/shard_map/cond/branch_1_fun/while/body/eval_jaxpr/hdq,hdk->hqk/dot_general | solution.py:73
  383.0 7.6 %multiply_convert_fusion.3 = bf16[12,512,512]{1,2,0:T(8,128)(2,1)S(1)} fusion(f32[12,512,512]{1,2,0:T(8,128)} %get-tuple-element.873, f32[12,512,512]{1,2,0:T(8,128)S(1)} %bitcast.242, f32[12,512]{1,0:T(8,128)S(1)} %get-tuple-element.872, f32[12,512]{1,0:T(8,128)S(1)} %log_add_fusion.1, pred[512]{0:T(512)(128)(4,1)S(1)} %iota_compare_fusion.1), kind=kLoop, calls=%fused_computation.74 | loop fusion | flops 18874368 | bytes 31506944 | tf_op jit(solution)/shard_map/cond/branch_1_fun/while/body/eval_jaxpr/convert_element_type | solution.py:80
  396.8 3.2 convert_reduce_fusion.8
  402.8 4.2 bitcast_add_fusion.4
  406.9 3.9 bitcast_add_fusion.3
  410.9 4.8 bitcast_add_fusion.2
  415.7 7.5 bitcast_add_fusion.1
  423.3 7.4 bitcast_add_fusion
  442.0 7.7 %copy.106 = bf16[768,3072]{1,0:T(8,128)(2,1)} copy(f32[768,3072]{0,1:T(8,128)} %get-tuple-element.589) | data formatting | bytes 14155776 | tf_op jit(solution)/shard_map/cond | solution.py:328
  449.8 7.7 %copy.107 = bf16[3072,768]{1,0:T(8,128)(2,1)} copy(f32[3072,768]{0,1:T(8,128)} %get-tuple-element.591) | data formatting | bytes 14155776 | tf_op jit(solution)/shard_map/cond | solution.py:328
  457.6 7.9 %reduce-scatter.7.cloned.1.call-done = bf16[96,768]{1,0:T(8,128)(2,1)} async-done(((bf16[768,768]{1,0:T(8,128)(2,1)}), bf16[96,768]{1,0:T(8,128)(2,1)}) %reduce-scatter.7.cloned.1.call-update) | async-done | bytes 147472 | tf_op jit(solution)/shard_map/reduce_scatter | solution.py:332
  465.5 34.0 %reduce-scatter.9.cloned.1.call-done = bf16[96,768]{1,0:T(8,128)(2,1)} async-done(((bf16[768,768]{1,0:T(8,128)(2,1)}), bf16[96,768]{1,0:T(8,128)(2,1)}) %reduce-scatter.9.cloned.1.call-update) | async-done | bytes 147472 | tf_op jit(solution)/shard_map/reduce_scatter | solution.py:332
  499.5 34.0 %reduce-scatter.11.cloned.1.call-done = bf16[96,768]{1,0:T(8,128)(2,1)} async-done(((bf16[768,768]{1,0:T(8,128)(2,1)}), bf16[96,768]{1,0:T(8,128)(2,1)}) %reduce-scatter.11.cloned.1.call-update) | async-done | bytes 147472 | tf_op jit(solution)/shard_map/reduce_scatter | solution.py:332
  533.6 33.9 %reduce-scatter.13.cloned.1.call-done = bf16[96,768]{1,0:T(8,128)(2,1)} async-done(((bf16[768,768]{1,0:T(8,128)(2,1)}), bf16[96,768]{1,0:T(8,128)(2,1)}) %reduce-scatter.13.cloned.1.call-update) | async-done | bytes 147472 | tf_op jit(solution)/shard_map/reduce_scatter | solution.py:332
  567.5 55.4 %reduce-scatter.15.cloned.1.call-done = bf16[96,3072]{1,0:T(8,128)(2,1)} async-done(((bf16[768,3072]{1,0:T(8,128)(2,1)}), bf16[96,3072]{1,0:T(8,128)(2,1)}) %reduce-scatter.15.cloned.1.call-update) | async-done | bytes 589840 | tf_op jit(solution)/shard_map/reduce_scatter | solution.py:332
  622.8 55.5 %reduce-scatter.17.cloned.1.call-done = bf16[384,768]{1,0:T(8,128)(2,1)} async-done(((bf16[3072,768]{1,0:T(8,128)(2,1)}), bf16[384,768]{1,0:T(8,128)(2,1)}) %reduce-scatter.17.cloned.1.call-update) | async-done | bytes 589840 | tf_op jit(solution)/shard_map/reduce_scatter | solution.py:332
  680.1 26.0 %all-reduce.17 = (bf16[768]{0:T(1024)(128)(2,1)S(1)}, bf16[768]{0:T(1024)(128)(2,1)S(1)}, bf16[768]{0:T(1024)(128)(2,1)S(1)}, bf16[768]{0:T(1024)(128)(2,1)S(1)}...) all-reduce(bf16[768]{0:T(1024)(128)(2,1)S(1)} %dynamic-update-slice, ...), channel_id=1, replica_groups=mesh['dp'=4,'fsdp'=8] {'fsdp'}, use_global_device_ids=true, to_apply=%add.7 | all-reduce | flops 9984 | bytes 39936
  706.8 10.0 %all-reduce.19 = (bf16[96]{0:T(256)(128)(2,1)S(1)}, bf16[96]{0:T(256)(128)(2,1)S(1)}, bf16[96]{0:T(256)(128)(2,1)S(1)}, bf16[96]{0:T(256)(128)(2,1)S(1)}, bf16[9...) all-reduce(bf16[96]{0:T(256)(128)(2,1)S(1)} %dynamic-slice.17, ...), channel_id=1, replica_groups=mesh['dp'=4,'fsdp'=8] {'dp'}, use_global_device_ids=true, to_apply=%region_47.48 | all-reduce | flops 1152 | bytes 4608 | tf_op jit(solution)/shard_map/psum | solution.py:335
  725.9 19.7 %all-reduce.23.cloned.1.call-done = (bf16[96,768]{1,0:T(8,128)(2,1)}, bf16[96,768]{1,0:T(8,128)(2,1)}, bf16[96,768]{1,0:T(8,128)(2,1)}, bf16[96,768]{1,0:T(8,128...) async-done(((bf16[96,768]{1,0:T(8,128)(2,1)}, bf16[96,768]{1,0:T(8,128)(2,1)}, bf16[96,768]{1,0:T(8,128)(2,1)}, bf16[96,768]{1,0:T(8,128)(2,1)}, ...) | async-done | bytes 1769488 | tf_op jit(solution)/shard_map/psum | solution.py:335
  (434 shorter events, 122.9 us)
Async XLA Ops:
  7.2 66.0 %copy-start.54 = (bf16[1024,768]{1,0:T(8,128)(2,1)S(1)}, bf16[1024,768]{1,0:T(8,128)(2,1)}, u32[]{:S(2)}) copy-start(bf16[1024,768]{1,0:T(8,128)(2,1)} %param.23) | copy-start | bytes 4718596
  7.2 66.0 %all-gather.8.cloned.1.call-start = ((), (), s32[]{:S(2)}) async-start(), calls=%async_computation.6 | async-start | bytes 1327104 | tf_op jit(solution)/shard_map/all_gather | solution.py:300
  7.9 67.7 %all-gather.10.cloned.1.call-start = ((), (), s32[]{:S(2)}) async-start(), calls=%async_computation.7 | async-start | bytes 1327104 | tf_op jit(solution)/shard_map/all_gather | solution.py:297
  8.7 75.0 %all-gather.12.cloned.1.call-start = ((), (), s32[]{:S(2)}) async-start(), calls=%async_computation.8 | async-start | bytes 1327104 | tf_op jit(solution)/shard_map/all_gather | solution.py:299
  9.4 98.2 %all-gather.14.cloned.1.call-start = ((), (), s32[]{:S(2)}) async-start(), calls=%async_computation.9 | async-start | bytes 1327104 | tf_op jit(solution)/shard_map/all_gather | solution.py:302
  10.0 150.0 %all-gather.16.cloned.1.call-start = ((), (), s32[]{:S(2)}) async-start(), calls=%async_computation.10 | async-start | bytes 5308416 | tf_op jit(solution)/shard_map/all_gather | solution.py:306
  10.6 200.9 %all-gather.18.cloned.1.call-start = ((), (), s32[]{:S(2)}) async-start(), calls=%async_computation.11 | async-start | bytes 5308416 | tf_op jit(solution)/shard_map/all_gather | solution.py:308
  11.2 454.4 %reduce-scatter.7.cloned.1.call-start = ((), (), s32[]{:S(2)}) async-start(), calls=%async_computation.12 | async-start | bytes 1327104 | tf_op jit(solution)/shard_map/reduce_scatter | solution.py:332
  53.0 20.3 %copy-start.92 = (bf16[768]{0:T(1024)(128)(2,1)}, bf16[768]{0:T(1024)(128)(2,1)S(1)}, u32[]{:S(2)}) copy-start(bf16[768]{0:T(1024)(128)(2,1)S(1)} %get-tuple-element.826) | copy-start | bytes 4612
  75.6 16.4 %copy-start.40 = (bf16[512,768]{0,1:T(8,128)(2,1)}, bf16[512,768]{0,1:T(8,128)(2,1)S(1)}, u32[]{:S(2)}) copy-start(bf16[512,768]{0,1:T(8,128)(2,1)S(1)} %copy.92) | copy-start | bytes 2359300
  92.0 18.3 %copy-start.36 = (bf16[768,768]{1,0:T(8,128)(2,1)S(1)}, bf16[768,768]{1,0:T(8,128)(2,1)}, u32[]{:S(2)}) copy-start(bf16[768,768]{1,0:T(8,128)(2,1)} %all-gather.8.cloned.1.call-done) | copy-start | bytes 3538948
  110.2 13.3 %copy-start.34 = (f32[512,768]{1,0:T(8,128)}, f32[512,768]{1,0:T(8,128)S(1)}, u32[]{:S(2)}) copy-start(f32[512,768]{1,0:T(8,128)S(1)} %get-tuple-element.897) | copy-start | bytes 4718596
  136.5 74.9 %copy-start.32 = (f32[512,768]{1,0:T(8,128)}, f32[512,768]{1,0:T(8,128)S(1)}, u32[]{:S(2)}) copy-start(f32[512,768]{1,0:T(8,128)S(1)} %get-tuple-element.853) | copy-start | bytes 4718596
  136.5 99.9 %copy-start.30 = (f32[512,768]{1,0:T(8,128)}, f32[512,768]{1,0:T(8,128)S(1)}, u32[]{:S(2)}) copy-start(f32[512,768]{1,0:T(8,128)S(1)} %get-tuple-element.889) | copy-start | bytes 4718596
  217.6 18.8 %copy-start.10 = (f32[512,768]{1,0:T(8,128)}, f32[512,768]{1,0:T(8,128)S(1)}, u32[]{:S(2)}) copy-start(f32[512,768]{1,0:T(8,128)S(1)} %get-tuple-element.905) | copy-start | bytes 4718596
  217.6 18.8 %copy-start.79 = (f32[512]{0:T(512)}, f32[512]{0:T(512)S(1)}, u32[]{:S(2)}) copy-start(f32[512]{0:T(512)S(1)} %broadcast_multiply_fusion.10) | copy-start | bytes 6148
  218.0 18.5 %copy-start.83 = (f32[512]{0:T(512)}, f32[512]{0:T(512)S(1)}, u32[]{:S(2)}) copy-start(f32[512]{0:T(512)S(1)} %add_rsqrt_fusion.6) | copy-start | bytes 6148
  218.0 18.5 %slice-start.8 = ((s8[4718592]{0:T(1024)(128)(4,1)}), s8[4194304]{0:T(1024)(128)(4,1)S(1)}, s32[]{:S(2)}) async-start(s8[4718592]{0:T(1024)(128)(4,1)} %bitcast.287), calls=%async_computation.27 | async-start | bytes 8388608
  218.0 23.2 %slice-start.12 = ((s8[6291456]{0:T(1024)(128)(4,1)}), s8[4194304]{0:T(1024)(128)(4,1)S(1)}, s32[]{:S(2)}) async-start(s8[6291456]{0:T(1024)(128)(4,1)} %bitcast.291), calls=%async_computation.31 | async-start | bytes 8388608
  218.2 18.2 %slice-start.9 = ((s8[4718592]{0:T(1024)(128)(4,1)}), s8[524288]{0:T(1024)(128)(4,1)S(1)}, s32[]{:S(2)}) async-start(s8[4718592]{0:T(1024)(128)(4,1)} %bitcast.287), calls=%async_computation.28 | async-start | bytes 1048576
  218.2 23.0 %slice-start.13 = ((s8[6291456]{0:T(1024)(128)(4,1)}), s8[2097152]{0:T(1024)(128)(4,1)S(1)}, s32[]{:S(2)}) async-start(s8[6291456]{0:T(1024)(128)(4,1)} %bitcast.291), calls=%async_computation.32 | async-start | bytes 4194304
  241.3 91.5 %copy-start.1 = (bf16[512,768]{0,1:T(8,128)(2,1)S(1)}, bf16[512,768]{0,1:T(8,128)(2,1)}, u32[]{:S(2)}) copy-start(bf16[512,768]{0,1:T(8,128)(2,1)} %copy-done) | copy-start | bytes 2359300
  241.3 91.5 %copy-start.60 = (f32[12,512]{1,0:T(8,128)S(1)}, f32[12,512]{1,0:T(8,128)}, u32[]{:S(2)}) copy-start(f32[12,512]{1,0:T(8,128)} %copy-done.59) | copy-start | bytes 73732
  241.3 91.4 %copy-start.64 = (f32[12,512]{1,0:T(8,128)S(1)}, f32[12,512]{1,0:T(8,128)}, u32[]{:S(2)}) copy-start(f32[12,512]{1,0:T(8,128)} %copy-done.63) | copy-start | bytes 73732
  241.3 91.4 %copy-start.90 = (f32[512]{0:T(512)S(1)}, f32[512]{0:T(512)}, u32[]{:S(2)}) copy-start(f32[512]{0:T(512)} %copy-done.89) | copy-start | bytes 6148
  249.7 17.9 %copy-start.28 = (f32[512,768]{1,0:T(8,128)}, f32[512,768]{1,0:T(8,128)S(1)}, u32[]{:S(2)}) copy-start(f32[512,768]{1,0:T(8,128)S(1)} %get-tuple-element.845) | copy-start | bytes 4718596 | tf_op jit(solution)/shard_map/cond
  271.1 33.7 %copy-start.9 = (f32[512,768]{1,0:T(8,128)}, f32[512,768]{1,0:T(8,128)S(1)}, u32[]{:S(2)}) copy-start(f32[512,768]{1,0:T(8,128)S(1)} %get-tuple-element.847) | copy-start | bytes 4718596 | tf_op jit(solution)/shard_map/cond
  342.5 18.8 %slice-start.6 = ((s8[4718592]{0:T(1024)(128)(4,1)}), s8[4194304]{0:T(1024)(128)(4,1)S(1)}, s32[]{:S(2)}) async-start(s8[4718592]{0:T(1024)(128)(4,1)} %bitcast.285), calls=%async_computation.25 | async-start | bytes 8388608 | tf_op jit(solution)/shard_map/cond
  343.4 17.8 %copy-start.26 = (f32[512,768]{1,0:T(8,128)}, f32[512,768]{1,0:T(8,128)S(1)}, u32[]{:S(2)}) copy-start(f32[512,768]{1,0:T(8,128)S(1)} %get-tuple-element.849) | copy-start | bytes 4718596 | tf_op jit(solution)/shard_map/cond
  343.5 17.8 %copy-start.31 = (f32[512,768]{1,0:T(8,128)S(1)}, f32[512,768]{1,0:T(8,128)}, u32[]{:S(2)}) copy-start(f32[512,768]{1,0:T(8,128)} %get-tuple-element.484) | copy-start | bytes 4718596 | tf_op jit(solution)/shard_map/cond
  343.5 17.8 %slice-start.7 = ((s8[4718592]{0:T(1024)(128)(4,1)}), s8[524288]{0:T(1024)(128)(4,1)S(1)}, s32[]{:S(2)}) async-start(s8[4718592]{0:T(1024)(128)(4,1)} %bitcast.285), calls=%async_computation.26 | async-start | bytes 1048576 | tf_op jit(solution)/shard_map/cond
  369.9 13.1 %slice-start.5 = ((s8[12582912]{0:T(1024)(128)(4,1)}), s8[4194304]{0:T(1024)(128)(4,1)S(1)}, s32[]{:S(2)}) async-start(s8[12582912]{0:T(1024)(128)(4,1)} %bitcast.241), calls=%async_computation.24 | async-start | bytes 8388608 | tf_op jit(solution)/shard_map/cond
  433.6 65.9 %reduce-scatter.9.cloned.1.call-start = ((), (), s32[]{:S(2)}) async-start(), calls=%async_computation.13 | async-start | bytes 1327104 | tf_op jit(solution)/shard_map/reduce_scatter | solution.py:332
  436.4 97.1 %reduce-scatter.11.cloned.1.call-start = ((), (), s32[]{:S(2)}) async-start(), calls=%async_computation.14 | async-start | bytes 1327104 | tf_op jit(solution)/shard_map/reduce_scatter | solution.py:332
  439.2 128.3 %reduce-scatter.13.cloned.1.call-start = ((), (), s32[]{:S(2)}) async-start(), calls=%async_computation.15 | async-start | bytes 1327104 | tf_op jit(solution)/shard_map/reduce_scatter | solution.py:332
  441.9 180.9 %reduce-scatter.15.cloned.1.call-start = ((), (), s32[]{:S(2)}) async-start(), calls=%async_computation.16 | async-start | bytes 5308416 | tf_op jit(solution)/shard_map/reduce_scatter | solution.py:332
  449.7 228.7 %reduce-scatter.17.cloned.1.call-start = ((), (), s32[]{:S(2)}) async-start(), calls=%async_computation.17 | async-start | bytes 5308416 | tf_op jit(solution)/shard_map/reduce_scatter | solution.py:332
  457.5 222.3 %copy-start.105 = (bf16[96]{0:T(256)(128)(2,1)S(1)}, bf16[96]{0:T(256)(128)(2,1)}, u32[]{:S(2)}) copy-start(bf16[96]{0:T(256)(128)(2,1)} %param.41) | copy-start | bytes 580
  457.5 222.6 %copy-start.70 = (f32[768]{0:T(1024)S(1)}, f32[768]{0:T(1024)}, u32[]{:S(2)}) copy-start(f32[768]{0:T(1024)} %get-tuple-element.592) | copy-start | bytes 9220
  457.5 222.6 %copy-start.74 = (f32[768]{0:T(1024)S(1)}, f32[768]{0:T(1024)}, u32[]{:S(2)}) copy-start(f32[768]{0:T(1024)} %get-tuple-element.593) | copy-start | bytes 9220
  457.5 222.6 %copy-start.78 = (f32[768]{0:T(1024)S(1)}, f32[768]{0:T(1024)}, u32[]{:S(2)}) copy-start(f32[768]{0:T(1024)} %get-tuple-element.594) | copy-start | bytes 9220
  457.5 264.0 %copy-start.11 = (f32[512,768]{1,0:T(8,128)S(1)}, f32[512,768]{1,0:T(8,128)}, u32[]{:S(2)}) copy-start(f32[512,768]{1,0:T(8,128)} %copy-done.10) | copy-start | bytes 4718596
  457.5 264.0 %copy-start.13 = (f32[512,768]{1,0:T(8,128)S(1)}, f32[512,768]{1,0:T(8,128)}, u32[]{:S(2)}) copy-start(f32[512,768]{1,0:T(8,128)} %copy-done.12) | copy-start | bytes 4718596
  457.5 264.0 %copy-start.80 = (f32[512]{0:T(512)S(1)}, f32[512]{0:T(512)}, u32[]{:S(2)}) copy-start(f32[512]{0:T(512)} %copy-done.79) | copy-start | bytes 6148
  457.5 264.0 %copy-start.82 = (f32[512]{0:T(512)S(1)}, f32[512]{0:T(512)}, u32[]{:S(2)}) copy-start(f32[512]{0:T(512)} %copy-done.81) | copy-start | bytes 6148
  457.5 264.0 %copy-start.84 = (f32[512]{0:T(512)S(1)}, f32[512]{0:T(512)}, u32[]{:S(2)}) copy-start(f32[512]{0:T(512)} %copy-done.83) | copy-start | bytes 6148
  457.5 264.0 %copy-start.86 = (f32[512]{0:T(512)S(1)}, f32[512]{0:T(512)}, u32[]{:S(2)}) copy-start(f32[512]{0:T(512)} %copy-done.85) | copy-start | bytes 6148
  457.6 288.0 %all-reduce.23.cloned.1.call-start = ((), (), s32[]{:S(2)}) async-start(), calls=%async_computation.18 | async-start | bytes 3538944 | tf_op jit(solution)/shard_map/psum | solution.py:335
  (87 other events, 414.2 us)
Sparse Core Ops, SparseCore 0:
  9.6 25.8 all-gather.7
  37.2 22.3 all-gather.9
  61.2 22.3 all-gather.11
  85.1 22.4 all-gather.13
  109.1 50.8 all-gather.15
  161.5 49.9 all-gather.17
  433.8 31.6 reduce-scatter.6
  468.4 31.1 reduce-scatter.8
  502.4 31.1 reduce-scatter.10
  536.3 31.1 reduce-scatter.12
  569.8 53.0 reduce-scatter.14
  625.0 53.3 reduce-scatter.16
  682.2 63.3 all-reduce.22
where the time goes:
time: 775 us; the launch traced here: 763 us
  waiting for transfers between devices  317 us (41%)
  matrix products  238 us (31%)
  blocking collectives  80.1 us (10%)
  other arithmetic  55.6 us (7%)
  local copies, waits for them, and re-layouts  52.5 us (7%)
  between operations  18.5 us (2%)
    reduce_scatter x6, waiting for transfers between devices, local(): lax.psum_scatter(for_sending(totals), 'fsdp', scatter_dimension=0, tiled=...  221 us
    dot_general x12, matrix products, project(): return jnp.dot(left, right, preferred_element_type=jnp.float32)  65.3 us
    unnamed x2, blocking collectives  57.4 us
    dot_general x12, matrix products, project_back(): jnp.einsum('rc,dc->rd', left, right, preferred_element_type=jnp.float32)  54.2 us
    dot_general x12, matrix products, weight_grad(): jnp.einsum('rc,rd->cd', left, right, preferred_element_type=jnp.float32)  53.8 us
    all_gather x1, waiting for transfers between devices, local(): lax.all_gather(shards[11], 'fsdp', axis=0, tiled=True)  32.7 us
    cond x6, local copies, waits for them, and re-layouts, local(): lax.cond(slot_index < group_count, run_backward, skip_backward, totals)  24.9 us
    dot_general x2, matrix products, attend_backward(): jnp.einsum('hdq,hdk->hqk', grad_cols, value_cols, preferred_element_type=...  23.5 us
  transfers between devices with their start and end apart: 13, of which 11 were waited for; matrix products, arithmetic and copies ran while one was open for 15% of the time, Pallas kernels for 0%

commit v1 on v0

--- a/solution.py
+++ b/solution.py
@@ -6,6 +6,27 @@
 HEADS = 12
 MB_CAP = 2
 norm_epsilon = 1e-05
+
+
+def joined_along(blocks, dim):
+    shape = list(blocks.shape[1:])
+    shape[dim] *= blocks.shape[0]
+    return jnp.moveaxis(blocks, 0, dim).reshape(shape)
+
+
+def doubled(x, axis):
+    size, index = (lax.axis_size(axis), lax.axis_index(axis))
+    blocks, apart = (x[None], 1)
+    while apart < size:
+        other = lax.ppermute(blocks, axis, [(i, i ^ apart) for i in range(size)])
+        low = index & apart == 0
+        blocks = jnp.concatenate([jnp.where(low, blocks, other), jnp.where(low, other, blocks)])
+        apart *= 2
+    return blocks
+
+
+def doubled_up(x, axis, dim):
+    return joined_along(doubled(x, axis), dim)
 
 
 def for_sending(shard):
@@ -303,7 +324,7 @@
             lax.all_gather(shards[6], "fsdp", axis=0, tiled=True),
             lax.all_gather(shards[7], "fsdp", axis=0, tiled=True),
             lax.all_gather(shards[8], "fsdp", axis=0, tiled=True),
-            lax.all_gather(shards[9], "fsdp", axis=0, tiled=True),
+            doubled_up(shards[9], "fsdp", 0),
             lax.all_gather(shards[10], "fsdp", axis=0, tiled=True),
             lax.all_gather(shards[11], "fsdp", axis=0, tiled=True),
             lax.all_gather(shards[12], "fsdp", axis=0, tiled=True),

time: 775 us -> 833 us (1.075)
  waiting for transfers between devices: 317 us -> 346 us
  blocking collectives: 80.1 us -> 98.5 us
  other arithmetic: 55.6 us -> 65.6 us
    ppermute x0 -> x3, waiting for transfers between devices: none -> 80.1 us  [doubled(): other = lax.ppermute(blocks, axis, [(i, i ^ apart) for i in range(size)])]
    all_gather x1, waiting for transfers between devices: 32.7 us -> 0.01 us  [local(): lax.all_gather(shards[11], 'fsdp', axis=0, tiled=True)]
    all_gather x1 -> x0, waiting for transfers between devices: 23.4 us -> none  [local(): lax.all_gather(shards[9], 'fsdp', axis=0, tiled=True)]
    unnamed x2, blocking collectives: 57.4 us -> 75.2 us
    all_gather x1, waiting for transfers between devices: 11.1 us -> 22.7 us  [local(): lax.all_gather(shards[5], 'fsdp', axis=0, tiled=True)]
  transfers between devices with their start and end apart: 13 -> 15, of which waited for: 11 -> 10; matrix products, arithmetic and copies ran while one was open for 15% -> 17% of each run, Pallas kernels for 0% -> 0%
where the time goes in v1:
time: 833 us; the launch traced here: 829 us
  waiting for transfers between devices  346 us (42%)
  matrix products  237 us (28%)
  blocking collectives  98.5 us (12%)
  other arithmetic  65.6 us (8%)
  local copies, waits for them, and re-layouts  56.9 us (7%)
  between operations  18.7 us (2%)
    reduce_scatter x6, waiting for transfers between devices, local(): lax.psum_scatter(for_sending(totals), 'fsdp', scatter_dimension=0, tiled=...  221 us
    ppermute x3, waiting for transfers between devices, doubled(): other = lax.ppermute(blocks, axis, [(i, i ^ apart) for i in range(size)])  80.1 us
    unnamed x2, blocking collectives  75.2 us
    dot_general x12, matrix products, project(): return jnp.dot(left, right, preferred_element_type=jnp.float32)  64.1 us
    dot_general x12, matrix products, weight_grad(): jnp.einsum('rc,rd->cd', left, right, preferred_element_type=jnp.float32)  53.9 us
    dot_general x12, matrix products, project_back(): jnp.einsum('rc,dc->rd', left, right, preferred_element_type=jnp.float32)  53.8 us
    cond x6, local copies, waits for them, and re-layouts, local(): lax.cond(slot_index < group_count, run_backward, skip_backward, totals)  25 us
    dot_general x2, matrix products, attend_backward(): jnp.einsum('hdq,hdk->hqk', grad_cols, value_cols, preferred_element_type=...  23.5 us
  transfers between devices with their start and end apart: 15, of which 10 were waited for; matrix products, arithmetic and copies ran while one was open for 17% of the time, Pallas kernels for 0%

profile of v1, /device:TPU:0, one launch (start us, length us, event | category | flops | bytes accessed | tf_op | source)
XLA Modules:
  0.0 829.3 jit_solution(17195513216065395185)
XLA Ops:
  27.5 49.1 %all-reduce.18 = (bf16[768]{0:T(1024)(128)(2,1)S(1)}, bf16[768]{0:T(1024)(128)(2,1)S(1)}, bf16[768]{0:T(1024)(128)(2,1)S(1)}, bf16[768]{0:T(1024)(128)(2,1)S(1)}...) all-reduce(bf16[768]{0:T(1024)(128)(2,1)S(1)} %dynamic-update-slice, ...), channel_id=1, replica_groups=mesh['dp'=4,'fsdp'=8] {'fsdp'}, use_global_device_ids=true, to_apply=%add | all-reduce | flops 5376 | bytes 21504
  78.6 13.4 %all-gather = bf16[8,1,384]{2,1,0:T(2,128)(2,1)S(1)} all-gather(bf16[1,1,384]{2,1,0:T(2,128)(2,1)S(1)} %reshape.286), channel_id=1, replica_groups=mesh['dp'=4,'fsdp'=8] {'fsdp'}, dimensions={0}, use_global_device_ids=true | all-gather | bytes 6912 | tf_op jit(solution)/shard_map/all_gather | solution.py:328
  96.2 3.7 slice_convert_fusion
  120.3 3.5 convolution_convert_fusion.2
  125.2 4.3 fusion.70
  132.4 4.2 fusion.97
  136.6 3.1 fusion.71
  142.9 3.3 fusion.96
  146.2 22.7 %all-gather.13.cloned.1.call-done = bf16[768,768]{1,0:T(8,128)(2,1)} async-done(((bf16[96,768]{1,0:T(8,128)(2,1)}), bf16[768,768]{1,0:T(8,128)(2,1)}) %all-gather.13.cloned.1.call-update) | async-done | bytes 1179664 | tf_op jit(solution)/shard_map/all_gather | solution.py:323
  174.8 78.3 %collective-permute-done.2 = bf16[4,96,3072]{2,1,0:T(8,128)(2,1)} collective-permute-done((bf16[4,96,3072]{2,1,0:T(8,128)(2,1)}, bf16[4,96,3072]{2,1,0:T(8,128)(2,1)}, u32[]{:S(2)}, u32[]{:S(2)}) %collective-permute-start.2) | collective-permute-done | bytes 2359328 | tf_op jit(solution)/shard_map/ppermute | solution.py:21
  255.7 18.7 %fusion.76 = (bf16[512,3072]{1,0:T(8,128)(2,1)}, f32[512,3072]{1,0:T(8,128)}) fusion(f32[3072]{0:T(1024)S(1)} %bitcast.292, bf16[512,768]{1,0:T(8,128)(2,1)S(1)} %get-tuple-element.852, bf16[768,3072]{1,0:T(8,128)(2,1)S(1)} %bitcast.259), kind=kOutput, calls=%fused_computation.162 | convolution fusion | flops 2519728128 | bytes 14954496 | tf_op jit(solution)/shard_map/dot_general | solution.py:114
  274.5 18.4 %fusion.79 = (bf16[512,3072]{1,0:T(8,128)(2,1)}, f32[512,3072]{1,0:T(8,128)}) fusion(f32[3072]{0:T(1024)S(1)} %bitcast.293, bf16[512,768]{1,0:T(8,128)(2,1)S(1)} %get-tuple-element.894, bf16[768,3072]{1,0:T(8,128)(2,1)S(1)} %bitcast.260), kind=kOutput, calls=%fused_computation.165 | convolution fusion | flops 2519728128 | bytes 14954496 | tf_op jit(solution)/shard_map/dot_general | solution.py:114
  292.9 6.1 fusion.115
  306.9 90.7 %conditional.2 = (bf16[512,768]{1,0:T(8,128)(2,1)}, f32[768,768]{0,1:T(8,128)S(1)}, f32[768]{0:T(1024)S(1)}, f32[768,768]{0,1:T(8,128)}, f32[768,768]{0,1:T(8,12...) conditional(s32[]{:T(128)} %bitcast.106, () %tuple.36, ...), branch_computations={%region_12.13_spmd, %region_13.28_spmd} | conditional | flops 16691619840 | bytes 337698560 | solution.py:349
  307.1 6.4 fusion.22
  315.2 17.5 %convert_reduce_fusion = (f32[3072]{0:T(1024)S(1)}, bf16[512,3072]{1,0:T(8,128)(2,1)S(1)}) fusion(f32[512,3072]{1,0:T(8,128)S(1)} %get-tuple-element.439, bf16[3072,768]{1,0:T(8,128)(2,1)S(1)} %get-tuple-element.440, f32[512,768]{1,0:T(8,128)S(1)} %get-tuple-element.845), kind=kOutput, calls=%fused_computation.10 | convolution fusion | flops 2532701184 | bytes 15740928 | tf_op jit(solution)/shard_map/cond/branch_1_fun/rc,dc->rd/dot_general | solution.py:118
  332.7 3.0 multiply_reduce_fusion.2
  340.3 11.7 %multiply_reduce_fusion = (f32[12,512]{1,0:T(8,128)S(1)}, f32[12,512,512]{1,2,0:T(8,128)}) fusion(f32[12,512,512]{1,2,0:T(8,128)} %fusion.22, f32[12,512]{1,0:T(8,128)S(1)} %log_add_fusion, pred[512]{0:T(512)(128)(4,1)S(1)} %iota_compare_fusion, bf16[12,64,512]{2,1,0:T(8,128)(2,1)} %bitcast.271, bf16[1,12,64,512]{3,2,1,0:T(8,128)(2,1)S(1)} %copy-done.40), kind=kOutput, calls=%fused_computation.1 | convolution fusion | flops 418375680 | bytes 26788352 | tf_op jit(solution)/shard_map/cond/branch_1_fun/while/body/eval_jaxpr/hdq,hdk->hqk/dot_general | solution.py:94
  353.1 7.4 multiply_convert_fusion
  366.7 3.2 convert_reduce_fusion.3
  372.6 3.6 convolution_bitcast_fusion.4
  376.2 3.6 convolution_bitcast_fusion.3
  379.8 3.9 convolution_bitcast_fusion.2
  383.7 8.4 %convolution_bitcast_fusion.1 = f32[768,3072]{0,1:T(8,128)} fusion(bf16[512,3072]{1,0:T(8,128)(2,1)} %copy-done.111, bf16[512,768]{1,0:T(8,128)(2,1)} %get-tuple-element.456), kind=kOutput, calls=%fused_computation.29 | convolution fusion | flops 2415919104 | bytes 13369344 | tf_op jit(solution)/shard_map/cond/branch_1_fun/rc,rd->cd/dot_general | solution.py:122
  392.1 5.0 convolution_bitcast_fusion
  398.2 99.2 %conditional.3 = (bf16[512,768]{1,0:T(8,128)(2,1)}, f32[768,768]{0,1:T(8,128)S(1)}, f32[768]{0:T(1024)S(1)}, f32[768,768]{0,1:T(8,128)}, f32[768,768]{0,1:T(8,12...) conditional(s32[]{:T(128)} %bitcast.112, ...), branch_computations={%region_28.29_spmd, %region_29.44_spmd} | conditional | flops 16698708992 | bytes 455893312 | solution.py:349
  398.2 7.7 fusion.57
  408.9 17.7 %convert_reduce_fusion.5 = (f32[3072]{0:T(1024)S(1)}, bf16[512,3072]{1,0:T(8,128)(2,1)S(1)}) fusion(f32[512,3072]{1,0:T(8,128)S(1)} %copy-done.112, bf16[3072,768]{1,0:T(8,128)(2,1)S(1)} %bitcast.299, f32[512,768]{1,0:T(8,128)S(1)} %get-tuple-element.849), kind=kOutput, calls=%fused_computation.86 | convolution fusion | flops 2532701184 | bytes 15740928 | tf_op jit(solution)/shard_map/cond/branch_1_fun/rc,dc->rd/dot_general | solution.py:118
  426.6 3.0 multiply_reduce_fusion.9
  435.3 11.8 %multiply_reduce_fusion.7 = (f32[12,512]{1,0:T(8,128)S(1)}, f32[12,512,512]{1,2,0:T(8,128)}) fusion(f32[12,512,512]{1,2,0:T(8,128)} %fusion.57, f32[12,512]{1,0:T(8,128)S(1)} %log_add_fusion.1, pred[512]{0:T(512)(128)(4,1)S(1)} %iota_compare_fusion.1, bf16[12,64,512]{2,1,0:T(8,128)(2,1)} %bitcast.273, bf16[1,12,64,512]{3,2,1,0:T(8,128)(2,1)} %get-tuple-element.491), kind=kOutput, calls=%fused_computation.75 | convolution fusion | flops 418375680 | bytes 26788352 | tf_op jit(solution)/shard_map/cond/branch_1_fun/while/body/eval_jaxpr/hdq,hdk->hqk/dot_general | solution.py:94
  448.3 7.4 multiply_convert_fusion.3
  461.9 3.2 convert_reduce_fusion.8
  467.9 4.2 bitcast_add_fusion.4
  472.1 3.9 bitcast_add_fusion.3
  476.0 4.8 bitcast_add_fusion.2
  480.9 7.5 bitcast_add_fusion.1
  488.5 7.4 bitcast_add_fusion
  507.2 7.7 copy.106
  515.0 7.7 copy.107
  522.8 7.9 reduce-scatter.7.cloned.1.call-done
  530.8 34.3 %reduce-scatter.9.cloned.1.call-done = bf16[96,768]{1,0:T(8,128)(2,1)} async-done(((bf16[768,768]{1,0:T(8,128)(2,1)}), bf16[96,768]{1,0:T(8,128)(2,1)}) %reduce-scatter.9.cloned.1.call-update) | async-done | bytes 147472 | tf_op jit(solution)/shard_map/reduce_scatter | solution.py:353
  565.1 34.1 %reduce-scatter.11.cloned.1.call-done = bf16[96,768]{1,0:T(8,128)(2,1)} async-done(((bf16[768,768]{1,0:T(8,128)(2,1)}), bf16[96,768]{1,0:T(8,128)(2,1)}) %reduce-scatter.11.cloned.1.call-update) | async-done | bytes 147472 | tf_op jit(solution)/shard_map/reduce_scatter | solution.py:353
  599.1 34.2 %reduce-scatter.13.cloned.1.call-done = bf16[96,768]{1,0:T(8,128)(2,1)} async-done(((bf16[768,768]{1,0:T(8,128)(2,1)}), bf16[96,768]{1,0:T(8,128)(2,1)}) %reduce-scatter.13.cloned.1.call-update) | async-done | bytes 147472 | tf_op jit(solution)/shard_map/reduce_scatter | solution.py:353
  633.3 55.3 %reduce-scatter.15.cloned.1.call-done = bf16[96,3072]{1,0:T(8,128)(2,1)} async-done(((bf16[768,3072]{1,0:T(8,128)(2,1)}), bf16[96,3072]{1,0:T(8,128)(2,1)}) %reduce-scatter.15.cloned.1.call-update) | async-done | bytes 589840 | tf_op jit(solution)/shard_map/reduce_scatter | solution.py:353
  688.6 55.7 %reduce-scatter.17.cloned.1.call-done = bf16[384,768]{1,0:T(8,128)(2,1)} async-done(((bf16[3072,768]{1,0:T(8,128)(2,1)}), bf16[384,768]{1,0:T(8,128)(2,1)}) %reduce-scatter.17.cloned.1.call-update) | async-done | bytes 589840 | tf_op jit(solution)/shard_map/reduce_scatter | solution.py:353
  746.0 26.0 %all-reduce.17 = (bf16[768]{0:T(1024)(128)(2,1)S(1)}, bf16[768]{0:T(1024)(128)(2,1)S(1)}, bf16[768]{0:T(1024)(128)(2,1)S(1)}, bf16[768]{0:T(1024)(128)(2,1)S(1)}...) all-reduce(bf16[768]{0:T(1024)(128)(2,1)S(1)} %dynamic-update-slice, ...), channel_id=1, replica_groups=mesh['dp'=4,'fsdp'=8] {'fsdp'}, use_global_device_ids=true, to_apply=%add.7 | all-reduce | flops 9984 | bytes 39936
  772.7 10.0 %all-reduce.19 = (bf16[96]{0:T(256)(128)(2,1)S(1)}, bf16[96]{0:T(256)(128)(2,1)S(1)}, bf16[96]{0:T(256)(128)(2,1)S(1)}, bf16[96]{0:T(256)(128)(2,1)S(1)}, bf16[9...) all-reduce(bf16[96]{0:T(256)(128)(2,1)S(1)} %dynamic-slice.17, ...), channel_id=1, replica_groups=mesh['dp'=4,'fsdp'=8] {'dp'}, use_global_device_ids=true, to_apply=%region_47.48 | all-reduce | flops 1152 | bytes 4608 | tf_op jit(solution)/shard_map/psum | solution.py:356
  791.8 19.5 %all-reduce.23.cloned.1.call-done = (bf16[96,768]{1,0:T(8,128)(2,1)}, bf16[96,768]{1,0:T(8,128)(2,1)}, bf16[96,768]{1,0:T(8,128)(2,1)}, bf16[96,768]{1,0:T(8,128...) async-done(((bf16[96,768]{1,0:T(8,128)(2,1)}, bf16[96,768]{1,0:T(8,128)(2,1)}, bf16[96,768]{1,0:T(8,128)(2,1)}, bf16[96,768]{1,0:T(8,128)(2,1)}, ...) | async-done | bytes 1769488 | tf_op jit(solution)/shard_map/psum | solution.py:356
  (453 shorter events, 135.5 us)
Async XLA Ops:
  7.2 89.0 %copy-start.53 = (bf16[1024,768]{1,0:T(8,128)(2,1)S(1)}, bf16[1024,768]{1,0:T(8,128)(2,1)}, u32[]{:S(2)}) copy-start(bf16[1024,768]{1,0:T(8,128)(2,1)} %param.24) | copy-start | bytes 4718596
  7.2 97.6 %all-gather.7.cloned.1.call-start = ((), (), s32[]{:S(2)}) async-start(), calls=%async_computation.6 | async-start | bytes 1327104 | tf_op jit(solution)/shard_map/all_gather | solution.py:321
  7.9 100.4 %all-gather.9.cloned.1.call-start = ((), (), s32[]{:S(2)}) async-start(), calls=%async_computation.7 | async-start | bytes 1327104 | tf_op jit(solution)/shard_map/all_gather | solution.py:318
  8.7 102.8 %all-gather.11.cloned.1.call-start = ((), (), s32[]{:S(2)}) async-start(), calls=%async_computation.8 | async-start | bytes 1327104 | tf_op jit(solution)/shard_map/all_gather | solution.py:320
  9.4 159.4 %all-gather.13.cloned.1.call-start = ((), (), s32[]{:S(2)}) async-start(), calls=%async_computation.9 | async-start | bytes 1327104 | tf_op jit(solution)/shard_map/all_gather | solution.py:323
  9.5 2.4 collective-permute-start
  10.0 282.8 %all-gather.15.cloned.1.call-start = ((), (), s32[]{:S(2)}) async-start(), calls=%async_computation.10 | async-start | bytes 5308416 | tf_op jit(solution)/shard_map/all_gather | solution.py:329
  14.1 85.7 %collective-permute-start.1 = (bf16[2,96,3072]{2,1,0:T(8,128)(2,1)}, bf16[2,96,3072]{2,1,0:T(8,128)(2,1)}, u32[]{:S(2)}, u32[]{:S(2)}) collective-permute-start(bf16[2,96,3072]{2,1,0:T(8,128)(2,1)} %pad_maximum_fusion.4), channel_id=1, source_target_pairs={{0,2},{1,3},{2,0},{3,1},{4,6},{5,7},{6,4},{7,5},{8,10},{9,11},{10,... | collective-permute-start | bytes 3538952 | tf_op jit(solution)/shard_map/ppermute | solution.py:21
  17.1 513.7 %reduce-scatter.7.cloned.1.call-start = ((), (), s32[]{:S(2)}) async-start(), calls=%async_computation.11 | async-start | bytes 1327104 | tf_op jit(solution)/shard_map/reduce_scatter | solution.py:353
  76.7 24.6 %copy-start.93 = (bf16[768]{0:T(1024)(128)(2,1)}, bf16[768]{0:T(1024)(128)(2,1)S(1)}, u32[]{:S(2)}) copy-start(bf16[768]{0:T(1024)(128)(2,1)S(1)} %get-tuple-element.826) | copy-start | bytes 4612
  103.9 149.1 %collective-permute-start.2 = (bf16[4,96,3072]{2,1,0:T(8,128)(2,1)}, bf16[4,96,3072]{2,1,0:T(8,128)(2,1)}, u32[]{:S(2)}, u32[]{:S(2)}) collective-permute-start(bf16[4,96,3072]{2,1,0:T(8,128)(2,1)} %pad_maximum_fusion.1), channel_id=1, source_target_pairs={{0,4},{1,5},{2,6},{3,7},{4,0},{5,1},{6,2},{7,3},{8,12},{9,13},{10,... | collective-permute-start | bytes 7077896 | tf_op jit(solution)/shard_map/ppermute | solution.py:21
  120.3 16.3 %copy-start.20 = (bf16[512,768]{0,1:T(8,128)(2,1)}, bf16[512,768]{0,1:T(8,128)(2,1)S(1)}, u32[]{:S(2)}) copy-start(bf16[512,768]{0,1:T(8,128)(2,1)S(1)} %copy.97) | copy-start | bytes 2359300
  142.9 26.0 %copy-start.55 = (bf16[1024,768]{1,0:T(8,128)(2,1)S(1)}, bf16[1024,768]{1,0:T(8,128)(2,1)}, u32[]{:S(2)}) copy-start(bf16[1024,768]{1,0:T(8,128)(2,1)} %param.23) | copy-start | bytes 4718596
  146.2 26.8 %copy-start.56 = (bf16[12,64,512]{2,1,0:T(8,128)(2,1)}, bf16[12,64,512]{2,1,0:T(8,128)(2,1)S(1)}, u32[]{:S(2)}) copy-start(bf16[12,64,512]{2,1,0:T(8,128)(2,1)S(1)} %fusion.96) | copy-start | bytes 2359300
  171.7 81.3 %copy-start.19 = (bf16[2,96,3072]{2,1,0:T(8,128)(2,1)S(1)}, bf16[2,96,3072]{2,1,0:T(8,128)(2,1)}, u32[]{:S(2)}) copy-start(bf16[2,96,3072]{2,1,0:T(8,128)(2,1)} %copy-done.18) | copy-start | bytes 3538948
  174.8 80.7 %copy-start.59 = (bf16[512,768]{1,0:T(8,128)(2,1)}, bf16[512,768]{1,0:T(8,128)(2,1)S(1)}, u32[]{:S(2)}) copy-start(bf16[512,768]{1,0:T(8,128)(2,1)S(1)} %get-tuple-element.852) | copy-start | bytes 2359300
  174.8 99.7 %copy-start.49 = (bf16[512,768]{1,0:T(8,128)(2,1)}, bf16[512,768]{1,0:T(8,128)(2,1)S(1)}, u32[]{:S(2)}) copy-start(bf16[512,768]{1,0:T(8,128)(2,1)S(1)} %get-tuple-element.894) | copy-start | bytes 2359300
  174.8 125.3 %copy-start.31 = (f32[512,768]{1,0:T(8,128)}, f32[512,768]{1,0:T(8,128)S(1)}, u32[]{:S(2)}) copy-start(f32[512,768]{1,0:T(8,128)S(1)} %get-tuple-element.895) | copy-start | bytes 4718596
  255.5 19.0 %copy-start.37 = (bf16[8,96,3072]{2,1,0:T(8,128)(2,1)}, bf16[8,96,3072]{2,1,0:T(8,128)(2,1)S(1)}, u32[]{:S(2)}) copy-start(bf16[8,96,3072]{2,1,0:T(8,128)(2,1)S(1)} %pad_maximum_fusion) | copy-start | bytes 14155780
  274.4 18.4 %copy-start.33 = (f32[512,768]{1,0:T(8,128)S(1)}, f32[512,768]{1,0:T(8,128)}, u32[]{:S(2)}) copy-start(f32[512,768]{1,0:T(8,128)} %get-tuple-element.853) | copy-start | bytes 4718596
  274.5 18.4 %copy-start.99 = (f32[768]{0:T(1024)S(1)}, f32[768]{0:T(1024)}, u32[]{:S(2)}) copy-start(f32[768]{0:T(1024)} %convert_element_type.408) | copy-start | bytes 9220
  306.8 91.3 %copy-start.1 = (bf16[512,768]{0,1:T(8,128)(2,1)S(1)}, bf16[512,768]{0,1:T(8,128)(2,1)}, u32[]{:S(2)}) copy-start(bf16[512,768]{0,1:T(8,128)(2,1)} %copy-done) | copy-start | bytes 2359300
  306.8 91.3 %copy-start.61 = (f32[12,512]{1,0:T(8,128)S(1)}, f32[12,512]{1,0:T(8,128)}, u32[]{:S(2)}) copy-start(f32[12,512]{1,0:T(8,128)} %copy-done.60) | copy-start | bytes 73732
  306.8 91.3 %copy-start.65 = (f32[12,512]{1,0:T(8,128)S(1)}, f32[12,512]{1,0:T(8,128)}, u32[]{:S(2)}) copy-start(f32[12,512]{1,0:T(8,128)} %copy-done.64) | copy-start | bytes 73732
  306.8 91.3 %copy-start.91 = (f32[512]{0:T(512)S(1)}, f32[512]{0:T(512)}, u32[]{:S(2)}) copy-start(f32[512]{0:T(512)} %copy-done.90) | copy-start | bytes 6148
  315.1 17.5 %copy-start.29 = (f32[512,768]{1,0:T(8,128)}, f32[512,768]{1,0:T(8,128)S(1)}, u32[]{:S(2)}) copy-start(f32[512,768]{1,0:T(8,128)S(1)} %get-tuple-element.845) | copy-start | bytes 4718596 | tf_op jit(solution)/shard_map/cond
  336.2 33.7 %copy-start.9 = (f32[512,768]{1,0:T(8,128)}, f32[512,768]{1,0:T(8,128)S(1)}, u32[]{:S(2)}) copy-start(f32[512,768]{1,0:T(8,128)S(1)} %get-tuple-element.847) | copy-start | bytes 4718596 | tf_op jit(solution)/shard_map/cond
  407.9 18.7 %slice-start.8 = ((s8[4718592]{0:T(1024)(128)(4,1)}), s8[4194304]{0:T(1024)(128)(4,1)S(1)}, s32[]{:S(2)}) async-start(s8[4718592]{0:T(1024)(128)(4,1)} %bitcast.265), calls=%async_computation.26 | async-start | bytes 8388608 | tf_op jit(solution)/shard_map/cond
  408.9 17.7 %copy-start.27 = (f32[512,768]{1,0:T(8,128)}, f32[512,768]{1,0:T(8,128)S(1)}, u32[]{:S(2)}) copy-start(f32[512,768]{1,0:T(8,128)S(1)} %get-tuple-element.849) | copy-start | bytes 4718596 | tf_op jit(solution)/shard_map/cond
  408.9 17.7 %copy-start.32 = (f32[512,768]{1,0:T(8,128)S(1)}, f32[512,768]{1,0:T(8,128)}, u32[]{:S(2)}) copy-start(f32[512,768]{1,0:T(8,128)} %get-tuple-element.484) | copy-start | bytes 4718596 | tf_op jit(solution)/shard_map/cond
  408.9 17.7 %slice-start.9 = ((s8[4718592]{0:T(1024)(128)(4,1)}), s8[524288]{0:T(1024)(128)(4,1)S(1)}, s32[]{:S(2)}) async-start(s8[4718592]{0:T(1024)(128)(4,1)} %bitcast.265), calls=%async_computation.27 | async-start | bytes 1048576 | tf_op jit(solution)/shard_map/cond
  435.3 13.1 %slice-start.5 = ((s8[12582912]{0:T(1024)(128)(4,1)}), s8[4194304]{0:T(1024)(128)(4,1)S(1)}, s32[]{:S(2)}) async-start(s8[12582912]{0:T(1024)(128)(4,1)} %bitcast.245), calls=%async_computation.23 | async-start | bytes 8388608 | tf_op jit(solution)/shard_map/cond
  498.9 66.2 %reduce-scatter.9.cloned.1.call-start = ((), (), s32[]{:S(2)}) async-start(), calls=%async_computation.12 | async-start | bytes 1327104 | tf_op jit(solution)/shard_map/reduce_scatter | solution.py:353
  501.6 97.5 %reduce-scatter.11.cloned.1.call-start = ((), (), s32[]{:S(2)}) async-start(), calls=%async_computation.13 | async-start | bytes 1327104 | tf_op jit(solution)/shard_map/reduce_scatter | solution.py:353
  504.4 128.9 %reduce-scatter.13.cloned.1.call-start = ((), (), s32[]{:S(2)}) async-start(), calls=%async_computation.14 | async-start | bytes 1327104 | tf_op jit(solution)/shard_map/reduce_scatter | solution.py:353
  507.2 181.4 %reduce-scatter.15.cloned.1.call-start = ((), (), s32[]{:S(2)}) async-start(), calls=%async_computation.15 | async-start | bytes 5308416 | tf_op jit(solution)/shard_map/reduce_scatter | solution.py:353
  515.0 229.3 %reduce-scatter.17.cloned.1.call-start = ((), (), s32[]{:S(2)}) async-start(), calls=%async_computation.16 | async-start | bytes 5308416 | tf_op jit(solution)/shard_map/reduce_scatter | solution.py:353
  522.7 222.9 %copy-start.110 = (bf16[96]{0:T(256)(128)(2,1)S(1)}, bf16[96]{0:T(256)(128)(2,1)}, u32[]{:S(2)}) copy-start(bf16[96]{0:T(256)(128)(2,1)} %param.41) | copy-start | bytes 580
  522.7 223.2 %copy-start.71 = (f32[768]{0:T(1024)S(1)}, f32[768]{0:T(1024)}, u32[]{:S(2)}) copy-start(f32[768]{0:T(1024)} %get-tuple-element.592) | copy-start | bytes 9220
  522.7 223.2 %copy-start.75 = (f32[768]{0:T(1024)S(1)}, f32[768]{0:T(1024)}, u32[]{:S(2)}) copy-start(f32[768]{0:T(1024)} %get-tuple-element.593) | copy-start | bytes 9220
  522.7 223.3 %copy-start.79 = (f32[768]{0:T(1024)S(1)}, f32[768]{0:T(1024)}, u32[]{:S(2)}) copy-start(f32[768]{0:T(1024)} %get-tuple-element.594) | copy-start | bytes 9220
  522.7 264.7 %copy-start.11 = (f32[512,768]{1,0:T(8,128)S(1)}, f32[512,768]{1,0:T(8,128)}, u32[]{:S(2)}) copy-start(f32[512,768]{1,0:T(8,128)} %copy-done.10) | copy-start | bytes 4718596
  522.7 264.7 %copy-start.13 = (f32[512,768]{1,0:T(8,128)S(1)}, f32[512,768]{1,0:T(8,128)}, u32[]{:S(2)}) copy-start(f32[512,768]{1,0:T(8,128)} %copy-done.12) | copy-start | bytes 4718596
  522.7 264.6 %copy-start.81 = (f32[512]{0:T(512)S(1)}, f32[512]{0:T(512)}, u32[]{:S(2)}) copy-start(f32[512]{0:T(512)} %copy-done.80) | copy-start | bytes 6148
  522.7 264.6 %copy-start.83 = (f32[512]{0:T(512)S(1)}, f32[512]{0:T(512)}, u32[]{:S(2)}) copy-start(f32[512]{0:T(512)} %copy-done.82) | copy-start | bytes 6148
  522.8 264.6 %copy-start.85 = (f32[512]{0:T(512)S(1)}, f32[512]{0:T(512)}, u32[]{:S(2)}) copy-start(f32[512]{0:T(512)} %copy-done.84) | copy-start | bytes 6148
  522.8 264.6 %copy-start.87 = (f32[512]{0:T(512)S(1)}, f32[512]{0:T(512)}, u32[]{:S(2)}) copy-start(f32[512]{0:T(512)} %copy-done.86) | copy-start | bytes 6148
  522.8 288.5 %all-reduce.23.cloned.1.call-start = ((), (), s32[]{:S(2)}) async-start(), calls=%async_computation.17 | async-start | bytes 3538944 | tf_op jit(solution)/shard_map/psum | solution.py:356
  (94 other events, 462.4 us)
Sparse Core Ops, SparseCore 0:
  9.6 31.6 all-gather.6
  43.0 24.6 all-gather.8
  69.3 22.5 all-gather.10
  93.3 75.4 all-gather.12
  170.3 70.1 all-gather.14
  499.0 31.7 reduce-scatter.6
  533.6 31.3 reduce-scatter.8
  567.9 31.1 reduce-scatter.10
  602.0 31.2 reduce-scatter.12
  635.4 53.1 reduce-scatter.14
  690.9 53.3 reduce-scatter.16
  747.9 63.3 all-reduce.22
